TPU v7x, 32 devices: a whole 2x2x4 slice. The times are simulated.
32 devices in a mesh: heads: 4 (over y, core), tokens: 4 (over z), cols: 2 (over x).
Axes of the slice: x: 2, y: 2, z: 4, core: 2. Of those that a mesh axis runs over, the one named last changes fastest.
Arguments:
- query_in: bfloat16 [2048, 8192], P('tokens', ('heads', 'cols')), may hold values from -24 to 24
- key_in: bfloat16 [2048, 8192], P('tokens', ('heads', 'cols')), may hold values from -24 to 24
- value_in: bfloat16 [2048, 8192], P('tokens', ('heads', 'cols')), may hold values from -6 to 6
- out_grads: bfloat16 [2048, 8192], P('tokens', ('heads', 'cols')), may hold values from -6 to 6
- doc_starts: int32 [6], replicated, may hold values from 0 to 2047, as said below
Outputs:
- input_factor: float32 [8192, 8192], P('heads', ('tokens', 'cols'))
- grad_factor: float32 [8192, 8192], P('heads', ('tokens', 'cols'))
Inputs may be any that keep to these rules, and one draw needn't show every extreme that they name: Strictly increasing with the first entry 0; document d runs from doc_starts[d] to the next start (the last one to 2048) - 1. One document holds (4 // 2 + 1) * 512 tokens.
All inputs are finite; a program needn't handle non-finite values.
Results may differ from a plain program's by a relative error of at most 0.0041.
Values may be sent and summed in bfloat16 or wider, within the bound.
A program may use at most 128 MiB of HBM per device.

v0:
```python
import math

import jax
import jax.numpy as jnp
from jax import lax
from jax.experimental import pallas as pl
from jax.experimental.pallas import tpu as pltpu
from jax.sharding import PartitionSpec as P

HEAD_DIM = 128


MASK_FLOOR = -1e30


def spread(value, axis, source):
    kept = jnp.where(lax.axis_index(axis) == source, value, 0).astype(value.dtype)
    return lax.psum(kept, axis)


def document_ids(positions, doc_starts):
    return jnp.sum((positions[:, None] >= doc_starts[None, :]).astype(jnp.int32), axis=1) - 1


def pair_scores(query_rows, key_rows, query_pos, key_pos, doc_starts):
    head_count = query_rows.shape[1] // HEAD_DIM
    query_heads = query_rows.reshape(query_rows.shape[0], head_count, HEAD_DIM)
    key_heads = key_rows.reshape(key_rows.shape[0], head_count, HEAD_DIM)
    scores = jnp.einsum(
        "qhd,khd->hqk", query_heads, key_heads, preferred_element_type=jnp.float32
    ) * (1.0 / math.sqrt(HEAD_DIM))
    query_docs = document_ids(query_pos, doc_starts)
    key_docs = document_ids(key_pos, doc_starts)
    allowed = query_docs[:, None] == key_docs[None, :]
    return (scores, allowed[None, :, :])


def on_device(query_in, key_in, value_in, out_grads, doc_starts):
    tok_dev, row_width = query_in.shape
    head_count = row_width // HEAD_DIM
    first_pos = lax.axis_index("tokens") * tok_dev
    query_pos = first_pos + jnp.arange(tok_dev, dtype=jnp.int32)
    keys_all, values_all = (
        lax.all_gather(key_in, "tokens", axis=0, tiled=True),
        lax.all_gather(value_in, "tokens", axis=0, tiled=True),
    )
    all_tokens = keys_all.shape[0]
    key_span = min(512, all_tokens)
    block_ids = jnp.arange(all_tokens // key_span, dtype=jnp.int32)

    def block_scores(block_id):
        key_begin = block_id * key_span
        key_rows = lax.dynamic_slice_in_dim(keys_all, key_begin, key_span, 0)
        key_pos = key_begin + jnp.arange(key_span, dtype=jnp.int32)
        scores, allowed = pair_scores(query_in, key_rows, query_pos, key_pos, doc_starts)
        return (key_begin, scores, allowed)

    def gated(block_id, update, running):
        key_begin = block_id * key_span
        return update(running)

    def stats_step(running, block_id):

        def update(state):
            row_peak, row_mass = state
            key_begin, scores, allowed = block_scores(block_id)
            masked = jnp.where(allowed, scores, MASK_FLOOR)
            new_peak = jnp.maximum(row_peak, jnp.max(masked, axis=2))
            new_mass = row_mass * jnp.exp(row_peak - new_peak) + jnp.sum(
                jnp.where(allowed, jnp.exp(masked - new_peak[:, :, None]), 0.0), axis=2
            )
            return (new_peak, new_mass)

        return (gated(block_id, update, running), None)

    initial = (
        jnp.full((head_count, tok_dev), MASK_FLOOR, jnp.float32),
        jnp.zeros((head_count, tok_dev), jnp.float32),
    )
    (row_peak, row_mass), _ = lax.scan(stats_step, initial, block_ids)
    log_total = row_peak + jnp.log(row_mass)

    def value_step(running, block_id):

        def update(state):
            weighted, partials = state
            key_begin, scores, allowed = block_scores(block_id)
            weights = jnp.where(allowed, jnp.exp(scores - log_total[:, :, None]), 0.0).astype(
                jnp.bfloat16
            )
            value_rows = lax.dynamic_slice_in_dim(values_all, key_begin, key_span, 0).reshape(
                key_span, head_count, HEAD_DIM
            )
            weighted = weighted + jnp.einsum(
                "hqk,khd->qhd", weights, value_rows, preferred_element_type=jnp.float32
            )
            return (weighted, partials)

        return (gated(block_id, update, running), None)

    partial_rows = 8
    value_init = (
        jnp.zeros((tok_dev, head_count, HEAD_DIM), jnp.float32),
        jnp.zeros((partial_rows, row_width), jnp.float32),
    )
    (weighted, partials), _ = lax.scan(value_step, value_init, block_ids)
    attended = weighted.reshape(tok_dev, row_width).astype(jnp.bfloat16)
    stats_all = lax.all_gather(log_total.T, "tokens", axis=0, tiled=True)
    query_rows = lax.all_gather(query_in, "tokens", axis=0, tiled=True)
    grad_rows = lax.all_gather(out_grads, "tokens", axis=0, tiled=True)
    piece_rows = query_rows.shape[0]
    piece_pos = jnp.arange(piece_rows, dtype=jnp.int32)

    def update(grad_sum):
        scores, allowed = pair_scores(query_rows, key_in, piece_pos, query_pos, doc_starts)
        weights = jnp.where(allowed, jnp.exp(scores - stats_all.T[:, :, None]), 0.0).astype(
            jnp.bfloat16
        )
        piece_grads = grad_rows.reshape(piece_rows, head_count, HEAD_DIM)
        return jnp.einsum("hqk,qhd->khd", weights, piece_grads, preferred_element_type=jnp.float32)

    summed = update(jnp.zeros((tok_dev, head_count, HEAD_DIM), jnp.float32))
    value_grads = summed.reshape(tok_dev, row_width).astype(jnp.bfloat16)
    token_shards = lax.axis_size("tokens")
    col_shards = lax.axis_size("cols")
    rows_attended, rows_grads = (
        lax.all_gather(attended[None], ("tokens", "cols"), axis=0, tiled=True),
        lax.all_gather(value_grads[None], ("tokens", "cols"), axis=0, tiled=True),
    )
    rows_attended = rows_attended.reshape(token_shards, col_shards, tok_dev, row_width)
    rows_grads = rows_grads.reshape(token_shards, col_shards, tok_dev, row_width)
    own_attended = lax.dynamic_index_in_dim(
        rows_attended, lax.axis_index("cols"), 1, keepdims=False
    )
    own_grads = lax.dynamic_index_in_dim(rows_grads, lax.axis_index("cols"), 1, keepdims=False)
    cols_attended, cols_grads = (
        spread(own_attended, "heads", lax.axis_index("tokens")),
        spread(own_grads, "heads", lax.axis_index("tokens")),
    )
    input_factor = jnp.einsum(
        "acnf,ang->cfg", rows_attended, cols_attended, preferred_element_type=jnp.float32
    )
    grad_factor = jnp.einsum(
        "acnf,ang->cfg", rows_grads, cols_grads, preferred_element_type=jnp.float32
    )
    input_factor = input_factor.reshape(col_shards * row_width, row_width) / all_tokens
    grad_factor = grad_factor.reshape(col_shards * row_width, row_width) / all_tokens
    return (input_factor, grad_factor)


BLOCK_Q = 256
SWAPPED = ((0, 1), (1, 0))
F32 = jnp.float32
BF16 = jnp.bfloat16


def fused_kernel(
    q_ref, k_ref, v_ref, g_ref, dk_ref, dq_ref, out_a, out_g,
    xin, rows, cols, v_t, g_acc, stage,
    own_sem, a2a_send, a2a_recv, row_recv, x_send, up_send, down_send,
    col_recv, pair_send, y_send, relay_send, swap_send, out_sem,
):
    n = lax.axis_size("tokens")
    tok_dev = q_ref.shape[0]
    all_tokens = n * tok_dev
    h = lax.axis_index("heads")
    z = lax.axis_index("tokens")
    x = lax.axis_index("cols")
    y = h // 2
    core = h % 2
    other_x = 1 - x
    pair = y * 2 + (1 - core)
    inputs = (q_ref, k_ref, v_ref, g_ref)

    barrier = pltpu.get_barrier_semaphore()
    for step in range(1, n):
        pl.semaphore_signal(barrier, inc=1, device_id={"tokens": (z + step) % n})
    for step in range(1, 4):
        pl.semaphore_signal(barrier, inc=1, device_id={"heads": (h + step) % 4})
    pl.semaphore_signal(barrier, inc=1, device_id={"cols": other_x})
    pl.semaphore_wait(barrier, n + 3)

    def a2a_copy(j, a, step):
        target = (z + step) % n
        return pltpu.make_async_remote_copy(
            src_ref=inputs[a].at[:, pl.ds(pl.multiple_of((j * n + target) * 128, 128), 128)],
            dst_ref=xin.at[j, a, pl.ds(pl.multiple_of(z * tok_dev, tok_dev), tok_dev), :],
            send_sem=a2a_send.at[j, a, step],
            recv_sem=a2a_recv.at[j, a, step],
            device_id={"tokens": target},
        )

    def own_copy(j, a):
        return pltpu.make_async_copy(
            inputs[a].at[:, pl.ds(pl.multiple_of((j * n + z) * 128, 128), 128)],
            xin.at[j, a, pl.ds(pl.multiple_of(z * tok_dev, tok_dev), tok_dev), :],
            own_sem.at[j, a],
        )

    def send_inputs(j):
        for a in range(4):
            for step in (2, 1, 3):
                a2a_copy(j, a, step).start()
            own_copy(j, a).start()

    def attention(j):
        for a in range(4):
            own_copy(j, a).wait()
            for step in range(1, n):
                a2a_copy(j, a, step).wait()
        if j == 0:
            send_inputs(1)
        v_t[...] = xin[j, 2].astype(F32).T.astype(BF16)
        g_acc[...] = jnp.zeros_like(g_acc)

        def block(ib, carry):
            span = pl.ds(pl.multiple_of(ib * BLOCK_Q, BLOCK_Q), BLOCK_Q)
            s = lax.dot_general(
                xin[j, 1], xin[j, 0, span, :], (((1,), (1,)), ((), ())),
                preferred_element_type=F32,
            ) * (1.0 / math.sqrt(HEAD_DIM))
            s = jnp.where(dk_ref[...] == dq_ref[:, span], s, MASK_FLOOR)
            e = jnp.exp(s - jnp.max(s, axis=0, keepdims=True))
            p = (e * (1.0 / jnp.sum(e, axis=0, keepdims=True))).astype(BF16)
            att = jnp.dot(v_t[...], p, preferred_element_type=F32)
            rows[j, 0, x, z, :, span] = att.astype(BF16)
            g_acc[...] += jnp.dot(p, xin[j, 3, span, :], preferred_element_type=F32)
            return carry

        lax.fori_loop(0, all_tokens // BLOCK_Q, block, 0)
        rows[j, 1, x, z] = g_acc[...].T.astype(BF16)

    def row_copy(j, f, xs, zs, send, device):
        piece = rows.at[j, f, xs, zs]
        return pltpu.make_async_remote_copy(
            src_ref=piece, dst_ref=piece, send_sem=send.at[j, f, zs],
            recv_sem=row_recv.at[j, f, xs, zs], device_id=device,
        )

    def x_copy(j, f, zs):
        return row_copy(j, f, x, zs, x_send, {"cols": other_x})

    def up_copy(j, f, zs):
        return row_copy(j, f, x, zs, up_send, {"tokens": (z + 1) % n})

    def down_copy(j, f, zs):
        return row_copy(j, f, x, zs, down_send, {"tokens": (z + n - 1) % n})

    def col_copy(j, f, zs, source, send, device):
        return pltpu.make_async_remote_copy(
            src_ref=source, dst_ref=cols.at[j, f, zs], send_sem=send.at[j, f, zs],
            recv_sem=col_recv.at[j, f, zs], device_id={"heads": device},
        )

    def pair_copy(j, f, zs):
        return col_copy(j, f, zs, rows.at[j, f, x, zs], pair_send, pair)

    def y_copy(j, f, zs):
        return col_copy(j, f, zs, rows.at[j, f, x, zs], y_send, (1 - y) * 2 + zs % 2)

    def relay_copy(j, f, zs):
        return col_copy(j, f, zs, cols.at[j, f, zs], relay_send, pair)

    mate = z + 1 - 2 * (z % 2)

    def swap_copy(j, f, zs):
        return row_copy(j, f, other_x, zs, swap_send, {"tokens": mate})

    def swap(j, f):
        x_copy_in = row_copy(j, f, other_x, z, x_send, {"cols": other_x})
        x_copy_in.wait_recv()
        swap_copy(j, f, z).start()

    def relay_x(j, f, zs):
        if (j, f) in SWAPPED:
            @pl.when(zs != mate)
            def _():
                x_copy(j, f, zs).start()
        else:
            x_copy(j, f, zs).start()

    is_source = h == z
    far = y != z // 2

    def feed_cols(j, f, zs):
        @pl.when(is_source)
        def _():
            pair_copy(j, f, zs).start()
            y_copy(j, f, zs).start()

    def send_own(j, f):
        @pl.when(z < n - 1)
        def _():
            up_copy(j, f, z).start()

        @pl.when(z > 0)
        def _():
            down_copy(j, f, z).start()

        x_copy(j, f, z).start()
        feed_cols(j, f, z)

    def relay_step(j, f, step):
        @pl.when(z >= step)
        def _():
            zs = z - step
            x_copy(j, f, zs).wait_recv()

            @pl.when(z < n - 1)
            def _():
                up_copy(j, f, zs).start()

            relay_x(j, f, zs)
            feed_cols(j, f, zs)

        @pl.when(z + step < n)
        def _():
            zs = z + step
            x_copy(j, f, zs).wait_recv()

            @pl.when(z > 0)
            def _():
                down_copy(j, f, zs).start()

            relay_x(j, f, zs)
            feed_cols(j, f, zs)

    def relay_cols(j, f):
        for zs in range(n):
            @pl.when(far & (core == zs % 2))
            def _():
                relay_copy(j, f, zs).wait_recv()
                relay_copy(j, f, zs).start()

    def finish_rows(j, f):
        def one(zs, carry):
            waiting = row_copy(j, f, other_x, zs, x_send, {"cols": other_x})
            if (j, f) in SWAPPED:
                @pl.when(zs != z)
                def _():
                    waiting.wait_recv()
            else:
                waiting.wait_recv()
            return carry

        lax.fori_loop(0, n, one, 0)

    def finish_cols(j, f):
        for zs in range(n):
            @pl.when((h != z) & jnp.logical_not(far & (core == zs % 2)))
            def _():
                relay_copy(j, f, zs).wait_recv()

        @pl.when(is_source)
        def _():
            def move(zs, carry):
                cols[j, f, zs] = rows[j, f, x, zs]
                return carry

            lax.fori_loop(0, n, move, 0)

    used = [0]
    span_rows = n * 128

    def out_copy(f, xs, jr, jc, slot):
        target = (out_a, out_g)[f]
        return pltpu.make_async_copy(
            stage.at[slot],
            target.at[
                pl.ds(pl.multiple_of(xs * (2 * span_rows) + jr * span_rows, span_rows), span_rows),
                pl.ds(jc * span_rows, span_rows),
            ],
            out_sem.at[slot],
        )

    def tiles(f, xs, jr, jc):
        slot = used[0] % 2
        if used[0] >= 2:
            out_copy(f, xs, jr, jc, slot).wait()
        used[0] += 1

        def part(m, carry):
            left = rows[jr, f, xs, pl.ds(2 * m, 2)].reshape(256, all_tokens)
            right = cols[jc, f].reshape(span_rows, all_tokens)
            stage[slot, pl.ds(pl.multiple_of(m * 256, 256), 256), :] = lax.dot_general(
                left, right, (((1,), (1,)), ((), ())), preferred_element_type=F32
            ) * (1.0 / all_tokens)
            return carry

        lax.fori_loop(0, n // 2, part, 0)
        out_copy(f, xs, jr, jc, slot).start()

    send_inputs(0)
    attention(0)
    send_own(0, 0)
    send_own(0, 1)

    def relay(j, f, step):
        relay_step(j, f, step)
        if step == 1 and (j, f) in SWAPPED:
            swap(j, f)

    relay(0, 0, 1)
    relay(0, 1, 1)
    attention(1)
    send_own(1, 0)
    send_own(1, 1)
    for f in range(2):
        for step in range(2, n):
            relay(0, f, step)
        relay_cols(0, f)
    for step in range(1, n):
        relay(1, 0, step)
    relay_cols(1, 0)
    early = []
    for f in range(2):
        finish_rows(0, f)
        finish_cols(0, f)
        early += [(f, x, 0, 0), (f, other_x, 0, 0)]
    for step in range(1, n):
        relay(1, 1, step)
        tiles(*early[step - 1])
    relay_cols(1, 1)
    for item in early[n - 1:]:
        tiles(*item)
    for f in range(2):
        finish_cols(1, f)
        for jr, jc in ((0, 1), (1, 0), (1, 1)):
            tiles(f, x, jr, jc)
        tiles(f, other_x, 0, 1)
        finish_rows(1, f)
        for jc in range(2):
            tiles(f, other_x, 1, jc)
    for slot in range(2):
        out_copy(0, x, 0, 0, slot).wait()

    for j in range(2):
        for f in range(2):
            for zs in range(n):
                if (j, f) in SWAPPED:
                    @pl.when(zs != mate)
                    def _():
                        x_copy(j, f, zs).wait_send()

                    @pl.when(zs == z)
                    def _():
                        swap_copy(j, f, zs).wait_send()
                else:
                    x_copy(j, f, zs).wait_send()

                @pl.when((z < n - 1) & (zs <= z))
                def _():
                    up_copy(j, f, zs).wait_send()

                @pl.when((z > 0) & (zs >= z))
                def _():
                    down_copy(j, f, zs).wait_send()

                @pl.when(is_source)
                def _():
                    pair_copy(j, f, zs).wait_send()
                    y_copy(j, f, zs).wait_send()

                @pl.when(far & (core == zs % 2))
                def _():
                    relay_copy(j, f, zs).wait_send()


def fused(query_in, key_in, value_in, out_grads, doc_starts):
    n = lax.axis_size("tokens")
    tok_dev, row_width = query_in.shape
    all_tokens = n * tok_dev
    docs = document_ids(jnp.arange(all_tokens, dtype=jnp.int32), doc_starts)
    dma = pltpu.SemaphoreType.DMA
    hbm = pl.BlockSpec(memory_space=pl.ANY)
    vmem = pl.BlockSpec(memory_space=pltpu.VMEM)
    out = jax.ShapeDtypeStruct((2 * row_width, row_width), F32)
    return tuple(pl.pallas_call(
        fused_kernel,
        out_shape=(out, out),
        in_specs=[hbm] * 4 + [vmem] * 2,
        out_specs=[hbm] * 2,
        scratch_shapes=[
            pltpu.VMEM((2, 4, all_tokens, HEAD_DIM), BF16),
            pltpu.VMEM((2, 2, 2, n, HEAD_DIM, all_tokens), BF16),
            pltpu.VMEM((2, 2, n, HEAD_DIM, all_tokens), BF16),
            pltpu.VMEM((HEAD_DIM, all_tokens), BF16),
            pltpu.VMEM((all_tokens, HEAD_DIM), F32),
            pltpu.VMEM((2, n * HEAD_DIM, n * HEAD_DIM), F32),
            dma((2, 4)), dma((2, 4, n)), dma((2, 4, n)),
            dma((2, 2, 2, n)), dma((2, 2, n)), dma((2, 2, n)), dma((2, 2, n)),
            dma((2, 2, n)), dma((2, 2, n)), dma((2, 2, n)), dma((2, 2, n)),
            dma((2, 2, n)), dma((2,)),
        ],
        compiler_params=pltpu.CompilerParams(
            collective_id=0, has_side_effects=True, vmem_limit_bytes=60 * 1024 * 1024
        ),
    )(query_in, key_in, value_in, out_grads, docs[:, None], docs[None, :]))


def per_device(query_in, key_in, value_in, out_grads, doc_starts):
    n = lax.axis_size("tokens")
    fits = n == 4 and lax.axis_size("heads") == 4 and lax.axis_size("cols") == 2
    if fits and query_in.shape[1] == 2 * n * HEAD_DIM and query_in.shape[0] % BLOCK_Q == 0:
        return fused(query_in, key_in, value_in, out_grads, doc_starts)
    return on_device(query_in, key_in, value_in, out_grads, doc_starts)


def solution(mesh):
    in_specs = (
        P("tokens", ("heads", "cols")),
        P("tokens", ("heads", "cols")),
        P("tokens", ("heads", "cols")),
        P("tokens", ("heads", "cols")),
        P(),
    )
    out_specs = (P("heads", ("tokens", "cols")), P("heads", ("tokens", "cols")))
    return jax.shard_map(
        per_device, mesh=mesh, in_specs=in_specs, out_specs=out_specs, check_vma=False
    )
```

profile of v0, /device:TPU:0, one launch (start us, length us, event | category | flops | bytes accessed | tf_op | source)
XLA Modules:
  0.0 290.9 jit_solution(14338880786466364013)
XLA Ops:
  0.6 0.7 convert_reduce_fusion
  1.4 0.0 copy-start.1
  1.4 1.3 copy.8.dk_ref
  2.8 0.0 copy-done.1
  2.8 276.1 %shard_map.68 = (f32[2048,1024]{1,0:T(8,128)}, f32[2048,1024]{1,0:T(8,128)}) custom-call(bf16[512,1024]{1,0:T(8,128)(2,1)} %q_ref.1, bf16[512,1024]{1,0:T(8,128)(2,1)} %k_ref.1, bf16[512,1024]{1,0:T(8,128)(2,1)} %v_ref.1, bf16[512,1024]{1,0:T(8,128)(2,1)} %g_ref.1, s32[2048,1]{1,0:T(8,128)} %copy.8.dk_ref, s32[1,2048]{1,0:T(1,128)} %bitcast.3), custom_call_target="tpu_custom_call" | custom-call | tf_op jit(solution)/shard_map/pallas_call | solution.py:478
  278.9 0.0 copy-start
  278.9 8.6 %copy.11 = f32[2048,1024]{1,0:T(8,128)} copy(f32[2048,1024]{1,0:T(8,128)} %get-tuple-element.4) | data formatting | bytes 16777216
  287.5 0.0 copy-done
  287.5 3.4 %copy.12 = f32[2048,1024]{1,0:T(8,128)} copy(f32[2048,1024]{1,0:T(8,128)S(1)} %copy-done) | data formatting | bytes 16777216
  (1 shorter events, 0.0 us)
Async XLA Ops:
  1.4 1.4 copy-start.1
  278.9 8.6 %copy-start = (f32[2048,1024]{1,0:T(8,128)S(1)}, f32[2048,1024]{1,0:T(8,128)}, u32[]{:S(2)}) copy-start(f32[2048,1024]{1,0:T(8,128)} %get-tuple-element.5) | copy-start | bytes 25165828
where the time goes:
time: 291 us
  Pallas kernels  276 us (95%)
  local copies, waits for them, and re-layouts  13.3 us (5%)
    pallas_call x1, Pallas kernels, fused(): pl.pallas_call(fused_kernel, out_shape=(out, out), in_specs=[hbm] * 4 + [...  276 us
    unnamed x6, local copies, waits for them, and re-layouts  12 us

commit v1 on v0

v1 whole, which is shorter than its diff:
```python
import math

import jax
import jax.numpy as jnp
from jax import lax
from jax.experimental import pallas as pl
from jax.experimental.pallas import tpu as pltpu
from jax.sharding import PartitionSpec as P

HEAD_DIM = 128


MASK_FLOOR = -1e30


def spread(value, axis, source):
    kept = jnp.where(lax.axis_index(axis) == source, value, 0).astype(value.dtype)
    return lax.psum(kept, axis)


def document_ids(positions, doc_starts):
    return jnp.sum((positions[:, None] >= doc_starts[None, :]).astype(jnp.int32), axis=1) - 1


def pair_scores(query_rows, key_rows, query_pos, key_pos, doc_starts):
    head_count = query_rows.shape[1] // HEAD_DIM
    query_heads = query_rows.reshape(query_rows.shape[0], head_count, HEAD_DIM)
    key_heads = key_rows.reshape(key_rows.shape[0], head_count, HEAD_DIM)
    scores = jnp.einsum(
        "qhd,khd->hqk", query_heads, key_heads, preferred_element_type=jnp.float32
    ) * (1.0 / math.sqrt(HEAD_DIM))
    query_docs = document_ids(query_pos, doc_starts)
    key_docs = document_ids(key_pos, doc_starts)
    allowed = query_docs[:, None] == key_docs[None, :]
    return (scores, allowed[None, :, :])


def on_device(query_in, key_in, value_in, out_grads, doc_starts):
    tok_dev, row_width = query_in.shape
    head_count = row_width // HEAD_DIM
    first_pos = lax.axis_index("tokens") * tok_dev
    query_pos = first_pos + jnp.arange(tok_dev, dtype=jnp.int32)
    keys_all, values_all = (
        lax.all_gather(key_in, "tokens", axis=0, tiled=True),
        lax.all_gather(value_in, "tokens", axis=0, tiled=True),
    )
    all_tokens = keys_all.shape[0]
    key_span = min(512, all_tokens)
    block_ids = jnp.arange(all_tokens // key_span, dtype=jnp.int32)

    def block_scores(block_id):
        key_begin = block_id * key_span
        key_rows = lax.dynamic_slice_in_dim(keys_all, key_begin, key_span, 0)
        key_pos = key_begin + jnp.arange(key_span, dtype=jnp.int32)
        scores, allowed = pair_scores(query_in, key_rows, query_pos, key_pos, doc_starts)
        return (key_begin, scores, allowed)

    def gated(block_id, update, running):
        key_begin = block_id * key_span
        return update(running)

    def stats_step(running, block_id):

        def update(state):
            row_peak, row_mass = state
            key_begin, scores, allowed = block_scores(block_id)
            masked = jnp.where(allowed, scores, MASK_FLOOR)
            new_peak = jnp.maximum(row_peak, jnp.max(masked, axis=2))
            new_mass = row_mass * jnp.exp(row_peak - new_peak) + jnp.sum(
                jnp.where(allowed, jnp.exp(masked - new_peak[:, :, None]), 0.0), axis=2
            )
            return (new_peak, new_mass)

        return (gated(block_id, update, running), None)

    initial = (
        jnp.full((head_count, tok_dev), MASK_FLOOR, jnp.float32),
        jnp.zeros((head_count, tok_dev), jnp.float32),
    )
    (row_peak, row_mass), _ = lax.scan(stats_step, initial, block_ids)
    log_total = row_peak + jnp.log(row_mass)

    def value_step(running, block_id):

        def update(state):
            weighted, partials = state
            key_begin, scores, allowed = block_scores(block_id)
            weights = jnp.where(allowed, jnp.exp(scores - log_total[:, :, None]), 0.0).astype(
                jnp.bfloat16
            )
            value_rows = lax.dynamic_slice_in_dim(values_all, key_begin, key_span, 0).reshape(
                key_span, head_count, HEAD_DIM
            )
            weighted = weighted + jnp.einsum(
                "hqk,khd->qhd", weights, value_rows, preferred_element_type=jnp.float32
            )
            return (weighted, partials)

        return (gated(block_id, update, running), None)

    partial_rows = 8
    value_init = (
        jnp.zeros((tok_dev, head_count, HEAD_DIM), jnp.float32),
        jnp.zeros((partial_rows, row_width), jnp.float32),
    )
    (weighted, partials), _ = lax.scan(value_step, value_init, block_ids)
    attended = weighted.reshape(tok_dev, row_width).astype(jnp.bfloat16)
    stats_all = lax.all_gather(log_total.T, "tokens", axis=0, tiled=True)
    query_rows = lax.all_gather(query_in, "tokens", axis=0, tiled=True)
    grad_rows = lax.all_gather(out_grads, "tokens", axis=0, tiled=True)
    piece_rows = query_rows.shape[0]
    piece_pos = jnp.arange(piece_rows, dtype=jnp.int32)

    def update(grad_sum):
        scores, allowed = pair_scores(query_rows, key_in, piece_pos, query_pos, doc_starts)
        weights = jnp.where(allowed, jnp.exp(scores - stats_all.T[:, :, None]), 0.0).astype(
            jnp.bfloat16
        )
        piece_grads = grad_rows.reshape(piece_rows, head_count, HEAD_DIM)
        return jnp.einsum("hqk,qhd->khd", weights, piece_grads, preferred_element_type=jnp.float32)

    summed = update(jnp.zeros((tok_dev, head_count, HEAD_DIM), jnp.float32))
    value_grads = summed.reshape(tok_dev, row_width).astype(jnp.bfloat16)
    token_shards = lax.axis_size("tokens")
    col_shards = lax.axis_size("cols")
    rows_attended, rows_grads = (
        lax.all_gather(attended[None], ("tokens", "cols"), axis=0, tiled=True),
        lax.all_gather(value_grads[None], ("tokens", "cols"), axis=0, tiled=True),
    )
    rows_attended = rows_attended.reshape(token_shards, col_shards, tok_dev, row_width)
    rows_grads = rows_grads.reshape(token_shards, col_shards, tok_dev, row_width)
    own_attended = lax.dynamic_index_in_dim(
        rows_attended, lax.axis_index("cols"), 1, keepdims=False
    )
    own_grads = lax.dynamic_index_in_dim(rows_grads, lax.axis_index("cols"), 1, keepdims=False)
    cols_attended, cols_grads = (
        spread(own_attended, "heads", lax.axis_index("tokens")),
        spread(own_grads, "heads", lax.axis_index("tokens")),
    )
    input_factor = jnp.einsum(
        "acnf,ang->cfg", rows_attended, cols_attended, preferred_element_type=jnp.float32
    )
    grad_factor = jnp.einsum(
        "acnf,ang->cfg", rows_grads, cols_grads, preferred_element_type=jnp.float32
    )
    input_factor = input_factor.reshape(col_shards * row_width, row_width) / all_tokens
    grad_factor = grad_factor.reshape(col_shards * row_width, row_width) / all_tokens
    return (input_factor, grad_factor)


TO_END = ((1, 1, 0), (1, 1, 1))
QUERY, KEY, VALUE, GRAD = range(4)
MATE, ACROSS, END = range(3)
F32 = jnp.float32
BF16 = jnp.bfloat16


def fused_kernel(
    starts_ref, q_ref, k_ref, v_ref, g_ref, out_a, out_g,
    xin, rows, cols, v_t, g_acc, key_doc, query_doc, stage,
    a2a_send, a2a_recv, row_recv, up_send, down_send, x_send, chunk_send, swap_send,
    col_recv, pair_send, y_send, relay_send, out_sem,
):
    n = lax.axis_size("tokens")
    tok_dev = q_ref.shape[0]
    all_tokens = n * tok_dev
    h = lax.axis_index("heads")
    z = lax.axis_index("tokens")
    x = lax.axis_index("cols")
    y = h // 2
    core = h % 2
    other_x = 1 - x
    pair = y * 2 + (1 - core)
    inputs = (q_ref, k_ref, v_ref, g_ref)
    half = HEAD_DIM // 2
    sources = (z + 1 - 2 * (z % 2), 2 - z // 2, 3 - 3 * (z // 2))

    barrier = pltpu.get_barrier_semaphore()
    for step in range(1, n):
        pl.semaphore_signal(barrier, inc=1, device_id={"tokens": (z + step) % n})
    for step in range(1, 4):
        pl.semaphore_signal(barrier, inc=1, device_id={"heads": (h + step) % 4})
    pl.semaphore_signal(barrier, inc=1, device_id={"cols": other_x})
    pl.semaphore_wait(barrier, n + 3)

    def feature_block(j, a, target):
        return inputs[a].at[:, pl.ds(pl.multiple_of((j * n + target) * HEAD_DIM, HEAD_DIM), HEAD_DIM)]

    def token_block(j, a, source):
        return xin.at[j, a, pl.ds(pl.multiple_of(source * tok_dev, tok_dev), tok_dev), :]

    def own_copy(j, a):
        return pltpu.make_async_copy(
            feature_block(j, a, z), token_block(j, a, z), a2a_recv.at[j, a, z]
        )

    def a2a_copy(j, a, source):
        target = sources[source]
        return pltpu.make_async_remote_copy(
            src_ref=feature_block(j, a, target), dst_ref=token_block(j, a, z),
            send_sem=a2a_send.at[j, a, source], recv_sem=a2a_recv.at[j, a, z],
            device_id={"tokens": target},
        )

    def arrived(j, a, position):
        block = token_block(j, a, position)
        pltpu.make_async_copy(block, block, a2a_recv.at[j, a, position]).wait()

    middle = (z > 0) & (z < n - 1)

    def send_inputs(j, kinds, targets):
        for source in targets:
            for a in kinds:
                a2a_copy(j, a, source).start()

    def send_own(j, kinds):
        for a in kinds:
            own_copy(j, a).start()

    def send_next(kinds):
        @pl.when(jnp.logical_not(middle))
        def _():
            send_inputs(1, kinds, (MATE,))

        for a in kinds:
            for source in (END, ACROSS):
                a2a_copy(1, a, source).start()

    def chunk_copy(position):
        piece = rows.at[0, 0, x, z, :, token_span(position)]
        return pltpu.make_async_remote_copy(
            src_ref=piece, dst_ref=piece, send_sem=chunk_send.at[position],
            recv_sem=row_recv.at[0, 0, x, z, 0], device_id={"cols": other_x},
        )

    def token_span(position):
        return pl.ds(pl.multiple_of(position * tok_dev, tok_dev), tok_dev)

    def attention(j, before, after):
        for position in (z,) + sources:
            arrived(j, VALUE, position)
        v_t[...] = xin[j, VALUE].astype(F32).T.astype(BF16)
        g_acc[...] = jnp.zeros_like(g_acc)

        def step(i, carry):
            position = jnp.where(i == 0, z, jnp.where(i == 1, sources[MATE], jnp.where(i == 2, sources[ACROSS], sources[END])))

            @pl.when(i == 2)
            def _():
                before()

            arrived(j, QUERY, position)
            arrived(j, GRAD, position)

            @pl.when(i == 2)
            def _():
                after()

            attention_block(j, position)
            if j == 0:
                chunk_copy(position).start()
            return carry

        lax.fori_loop(0, n, step, 0)
        rows[j, 1, x, z] = g_acc[...].T.astype(BF16)

    def attention_block(j, position):
        span = token_span(position)
        s = lax.dot_general(
            xin[j, KEY], xin[j, QUERY, span, :], (((1,), (1,)), ((), ())),
            preferred_element_type=F32,
        ) * (1.0 / math.sqrt(HEAD_DIM))
        s = jnp.where(key_doc[...] == query_doc[:, span], s, MASK_FLOOR)
        e = jnp.exp(s - jnp.max(s, axis=0, keepdims=True))
        p = (e * (1.0 / jnp.sum(e, axis=0, keepdims=True))).astype(BF16)
        att = jnp.dot(v_t[...], p, preferred_element_type=F32)
        rows[j, 0, x, z, :, span] = att.astype(BF16)
        g_acc[...] += jnp.dot(p, xin[j, GRAD, span, :], preferred_element_type=F32)

    def row_copy(j, f, xs, zs, part, send, device):
        piece = rows.at[j, f, xs, zs, pl.ds(part * half, half), :]
        return pltpu.make_async_remote_copy(
            src_ref=piece, dst_ref=piece, send_sem=send,
            recv_sem=row_recv.at[j, f, xs, zs, part], device_id=device,
        )

    over_x = {"cols": other_x}
    mate = sources[MATE]

    def up_copy(j, f, part, zs):
        return row_copy(j, f, x, zs, part, up_send.at[j, f, part, zs], {"tokens": (z + 1) % n})

    def down_copy(j, f, part, zs):
        return row_copy(j, f, x, zs, part, down_send.at[j, f, part, zs], {"tokens": (z + n - 1) % n})

    def x_copy(j, f, part, zs):
        return row_copy(j, f, x, zs, part, x_send.at[j, f, part, zs], over_x)

    def swap_copy(j, f, part):
        return row_copy(j, f, other_x, z, part, swap_send.at[j, f, part], {"tokens": mate})

    def own_rows(j, f):
        for part in range(2):
            @pl.when(z < n - 1)
            def _():
                up_copy(j, f, part, z).start()

            @pl.when(z > 0)
            def _():
                down_copy(j, f, part, z).start()

            if (j, f) != (0, 0):
                x_copy(j, f, part, z).start()
        feed_cols(j, f, z)

    def rows_in(j, f, source):
        zs = sources[source]
        for part in range(2):
            x_copy(j, f, part, zs).wait_recv()

            @pl.when((zs < z) & (z < n - 1))
            def _():
                up_copy(j, f, part, zs).start()

            @pl.when((zs > z) & (z > 0))
            def _():
                down_copy(j, f, part, zs).start()

            if source != MATE:
                x_copy(j, f, part, zs).start()
            elif (j, f, part) not in TO_END:
                @pl.when(jnp.logical_not(middle))
                def _():
                    x_copy(j, f, part, zs).start()
        feed_cols(j, f, zs)

    def other_in(j, f, source, part):
        zs = z if source is None else sources[source]
        if (j, f, source) == (0, 0, None):
            if part == 0:
                piece = rows.at[0, 0, other_x, z]
                pltpu.make_async_copy(piece, piece, row_recv.at[0, 0, other_x, z, 0]).wait()
            return
        row_copy(j, f, other_x, zs, part, x_send.at[j, f, part, zs], over_x).wait_recv()

    def swap_rows(j, f, parts):
        for part in parts:
            other_in(j, f, None, part)
        for part in parts:
            swap_copy(j, f, part).start()

    def swap_to_end():
        for j, f, part in TO_END:
            swap_rows(j, f, (part,))

    def other_rows(j, f, group):
        if group == (MATE,):
            for part in range(2):
                if (j, f, part) not in TO_END:
                    @pl.when(middle)
                    def _():
                        other_in(j, f, None, part)
        for source in group:
            for part in range(2):
                other_in(j, f, source, part)

    is_source = h == z
    far = y != z // 2

    def col_copy(j, f, zs, source, send, device):
        return pltpu.make_async_remote_copy(
            src_ref=source, dst_ref=cols.at[j, f, zs], send_sem=send.at[j, f, zs],
            recv_sem=col_recv.at[j, f, zs], device_id={"heads": device},
        )

    def pair_copy(j, f, zs):
        return col_copy(j, f, zs, rows.at[j, f, x, zs], pair_send, pair)

    def y_copy(j, f, zs):
        return col_copy(j, f, zs, rows.at[j, f, x, zs], y_send, (1 - y) * 2 + zs % 2)

    def relay_copy(j, f, zs):
        return col_copy(j, f, zs, cols.at[j, f, zs], relay_send, pair)

    def feed_cols(j, f, zs):
        @pl.when(is_source)
        def _():
            y_copy(j, f, zs).start()
            pair_copy(j, f, zs).start()

    def relay_cols(j, f, source):
        zs = z if source is None else sources[source]

        @pl.when(far & (core == zs % 2))
        def _():
            relay_copy(j, f, zs).wait_recv()
            relay_copy(j, f, zs).start()

    def cols_in(j, f, source):
        zs = z if source is None else sources[source]

        @pl.when(jnp.logical_not(is_source | (far & (core == zs % 2))))
        def _():
            relay_copy(j, f, zs).wait_recv()

        @pl.when(is_source)
        def _():
            cols[j, f, zs] = rows[j, f, x, zs]

    used = [0]
    wide = 2 * HEAD_DIM
    slots = stage.shape[0]

    def out_copy(f, row, col, slot):
        return pltpu.make_async_copy(
            stage.at[slot],
            (out_a, out_g)[f].at[
                pl.ds(pl.multiple_of(row * wide, wide), wide),
                pl.ds(pl.multiple_of(col * wide, wide), wide),
            ],
            out_sem.at[slot],
        )

    def products(f, xs, left, right):
        done = used[0]
        count = len(left) * len(right)

        def one(i, carry):
            at_left, at_right = i // len(right), i % len(right)
            jr = sum(((at_left == k) * item[0] for k, item in enumerate(left)), 0)
            pr = sum(((at_left == k) * item[1] for k, item in enumerate(left)), 0)
            jc = sum(((at_right == k) * item[0] for k, item in enumerate(right)), 0)
            pc = sum(((at_right == k) * item[1] for k, item in enumerate(right)), 0)
            slot = (done + i) % slots

            @pl.when(done + i >= slots)
            def _():
                out_copy(f, 0, 0, slot).wait()

            stage[slot] = (
                lax.dot_general(
                    rows[jr, f, xs, pl.ds(2 * pr, 2)].reshape(wide, all_tokens),
                    cols[jc, f, pl.ds(2 * pc, 2)].reshape(wide, all_tokens),
                    (((1,), (1,)), ((), ())), preferred_element_type=F32,
                ) * (1.0 / all_tokens)
            ).astype(stage.dtype)
            out_copy(f, 4 * xs + 2 * jr + pr, 2 * jc + pc, slot).start()
            return carry

        lax.fori_loop(0, count, one, 0)
        used[0] += count

    for a in (KEY, VALUE):
        send_inputs(0, (a,), (END, ACROSS))
    send_inputs(0, (KEY, VALUE), (MATE,))
    send_own(0, (KEY, VALUE, QUERY, GRAD))
    send_own(1, (KEY, VALUE, QUERY, GRAD))
    doc_count = starts_ref.shape[0]
    key_pos = lax.broadcasted_iota(jnp.int32, key_doc.shape, 0)
    query_pos = lax.broadcasted_iota(jnp.int32, query_doc.shape, 1)
    key_doc[...] = sum((key_pos >= starts_ref[d]).astype(jnp.int32) for d in range(doc_count))
    query_doc[...] = sum((query_pos >= starts_ref[d]).astype(jnp.int32) for d in range(doc_count))
    for position in (z,) + sources:
        arrived(0, KEY, position)
    send_inputs(0, (QUERY, GRAD), (MATE,))
    for a in (QUERY, GRAD):
        send_inputs(0, (a,), (END, ACROSS))

    @pl.when(middle)
    def _():
        send_inputs(1, (KEY, VALUE, QUERY, GRAD), (MATE,))

    def nothing():
        pass

    def send_rest():
        send_next((KEY, VALUE))
        send_next((QUERY, GRAD))

    def at_ends(j, f):
        @pl.when(jnp.logical_not(middle))
        def _():
            rows_in(j, f, MATE)

    def in_middle(j, f):
        @pl.when(middle)
        def _():
            rows_in(j, f, MATE)

    def end_swap(j, f):
        @pl.when(jnp.logical_not(middle))
        def _():
            swap_rows(j, f, range(2))

    attention(0, nothing, send_rest)
    own_rows(0, 0)
    own_rows(0, 1)
    at_ends(0, 0)
    for position in (z,) + sources:
        arrived(1, KEY, position)

    def gather_middle():
        in_middle(0, 0)

    def relay_pair(j, f, group):
        for source in group:
            relay_cols(j, f, source)

    def cols_pair(j, f, group):
        for source in group:
            cols_in(j, f, source)

    attention(1, lambda: at_ends(0, 1), gather_middle)
    near = z // 2
    first, last = (0, near), (0, 1 - near)
    second, final = (1, near), (1, 1 - near)
    own_rows(1, 0)
    own_rows(1, 1)
    in_middle(0, 1)
    at_ends(1, 0)
    end_swap(0, 0)
    end_swap(0, 1)
    at_ends(1, 1)
    rows_in(0, 0, ACROSS)
    in_middle(1, 0)
    end_swap(1, 0)
    rows_in(0, 1, ACROSS)
    in_middle(1, 1)
    end_swap(1, 1)
    relay_pair(0, 0, (None, MATE))
    relay_pair(0, 1, (None, MATE))
    rows_in(0, 0, END)
    relay_pair(1, 0, (None, MATE))
    relay_pair(1, 1, (None,))
    cols_pair(0, 0, (None, MATE))
    cols_pair(1, 0, (None, MATE))
    products(0, x, (first, second), (first, second))
    rows_in(0, 1, END)
    relay_pair(0, 0, (ACROSS,))
    relay_pair(0, 1, (ACROSS,))
    relay_pair(1, 1, (MATE,))
    cols_pair(0, 1, (None, MATE))
    cols_pair(1, 1, (None, MATE))
    products(1, x, (first, second), (first, second))
    rows_in(1, 0, ACROSS)
    relay_pair(0, 0, (END,))
    cols_pair(0, 0, (ACROSS, END))
    products(0, x, (last,), (first, second, last))
    products(0, x, (first, second), (last,))
    rows_in(1, 1, ACROSS)
    relay_pair(0, 1, (END,))
    relay_pair(1, 0, (ACROSS,))
    cols_pair(0, 1, (ACROSS, END))
    products(1, x, (last,), (first, second, last))
    products(1, x, (first, second), (last,))
    other_rows(0, 0, (MATE,))
    other_rows(1, 0, (MATE,))
    products(0, other_x, (first, second), (first, second, last))
    rows_in(1, 0, END)
    relay_pair(1, 1, (ACROSS,))
    other_rows(0, 1, (MATE,))
    products(1, other_x, (first,), (first, second, last))
    other_rows(0, 0, (ACROSS, END))
    products(0, other_x, (last,), (first, second, last))
    relay_pair(1, 0, (END,))
    cols_pair(1, 0, (ACROSS, END))
    products(0, x, (final,), (first, second, last, final))
    products(0, x, (first, second, last), (final,))
    rows_in(1, 1, END)

    @pl.when(middle)
    def _():
        swap_to_end()

    products(0, other_x, (first, second, last), (final,))
    other_rows(0, 1, (ACROSS, END))
    products(1, other_x, (last,), (first, second, last))
    products(1, x, (final,), (first, second, last))
    relay_pair(1, 1, (END,))
    other_rows(1, 0, (ACROSS, END))
    products(0, other_x, (final,), (first, second, last, final))
    cols_pair(1, 1, (ACROSS, END))
    products(1, x, (first, second, last, final), (final,))
    products(1, other_x, (first, last), (final,))
    other_rows(1, 1, (MATE,))
    products(1, other_x, (second,), (first, second, last, final))
    other_rows(1, 1, (ACROSS, END))
    products(1, other_x, (final,), (first, second, last, final))
    for slot in range(slots):
        out_copy(0, 0, 0, slot).wait()

    for j in range(2):
        for a in range(4):
            for source in range(3):
                a2a_copy(j, a, source).wait_send()
        for f in range(2):
            for part in range(2):
                def sent(zs, carry):
                    own_chunks = (zs == z) if (j, f) == (0, 0) else False
                    swapped = (zs == mate) if (j, f, part) in TO_END else (zs == mate) & middle

                    @pl.when(jnp.logical_not(swapped | own_chunks))
                    def _():
                        x_copy(j, f, part, zs).wait_send()

                    if (j, f, part) == (0, 0, 0):
                        chunk_copy(zs).wait_send()

                    @pl.when((z < n - 1) & (zs <= z))
                    def _():
                        up_copy(j, f, part, zs).wait_send()

                    @pl.when((z > 0) & (zs >= z))
                    def _():
                        down_copy(j, f, part, zs).wait_send()

                    return carry

                lax.fori_loop(0, n, sent, 0)
            for zs in range(n):
                @pl.when(is_source)
                def _():
                    pair_copy(j, f, zs).wait_send()
                    y_copy(j, f, zs).wait_send()

                @pl.when(far & (core == zs % 2))
                def _():
                    relay_copy(j, f, zs).wait_send()
    for j in range(2):
        for f in range(2):
            for part in range(2):
                if (j, f, part) in TO_END:
                    swap_copy(j, f, part).wait_send()
                else:
                    @pl.when(jnp.logical_not(middle))
                    def _():
                        swap_copy(j, f, part).wait_send()


def fused(query_in, key_in, value_in, out_grads, doc_starts):
    n = lax.axis_size("tokens")
    tok_dev, row_width = query_in.shape
    all_tokens = n * tok_dev
    dma = pltpu.SemaphoreType.DMA
    hbm = pl.BlockSpec(memory_space=pl.ANY)
    smem = pl.BlockSpec(memory_space=pltpu.SMEM)
    out = jax.ShapeDtypeStruct((2 * row_width, row_width), F32)
    return tuple(pl.pallas_call(
        fused_kernel,
        out_shape=(out, out),
        in_specs=[smem] + [hbm] * 4,
        out_specs=[hbm] * 2,
        scratch_shapes=[
            pltpu.VMEM((2, 4, all_tokens, HEAD_DIM), BF16),
            pltpu.VMEM((2, 2, 2, n, HEAD_DIM, all_tokens), BF16),
            pltpu.VMEM((2, 2, n, HEAD_DIM, all_tokens), BF16),
            pltpu.VMEM((HEAD_DIM, all_tokens), BF16),
            pltpu.VMEM((all_tokens, HEAD_DIM), F32),
            pltpu.VMEM((all_tokens, 1), jnp.int32),
            pltpu.VMEM((1, all_tokens), jnp.int32),
            pltpu.VMEM((8, 2 * HEAD_DIM, 2 * HEAD_DIM), F32),
            dma((2, 4, 3)), dma((2, 4, n)), dma((2, 2, 2, n, 2)),
            dma((2, 2, 2, n)), dma((2, 2, 2, n)), dma((2, 2, 2, n)), dma((n,)), dma((2, 2, 2)),
            dma((2, 2, n)), dma((2, 2, n)), dma((2, 2, n)), dma((2, 2, n)), dma((8,)),
        ],
        compiler_params=pltpu.CompilerParams(
            collective_id=0, has_side_effects=True, vmem_limit_bytes=60 * 1024 * 1024
        ),
    )(doc_starts, query_in, key_in, value_in, out_grads))


def per_device(query_in, key_in, value_in, out_grads, doc_starts):
    n = lax.axis_size("tokens")
    fits = n == 4 and lax.axis_size("heads") == 4 and lax.axis_size("cols") == 2
    if fits and query_in.shape[1] == 2 * n * HEAD_DIM and query_in.shape[0] % HEAD_DIM == 0:
        return fused(query_in, key_in, value_in, out_grads, doc_starts)
    return on_device(query_in, key_in, value_in, out_grads, doc_starts)


def solution(mesh):
    in_specs = (
        P("tokens", ("heads", "cols")),
        P("tokens", ("heads", "cols")),
        P("tokens", ("heads", "cols")),
        P("tokens", ("heads", "cols")),
        P(),
    )
    out_specs = (P("heads", ("tokens", "cols")), P("heads", ("tokens", "cols")))
    return jax.shard_map(
        per_device, mesh=mesh, in_specs=in_specs, out_specs=out_specs, check_vma=False
    )
```

time: 291 us -> 252 us (0.87)
  Pallas kernels: 276 us -> 237 us
    pallas_call x1, Pallas kernels: 276 us -> 237 us  [fused(): pl.pallas_call(fused_kernel, out_shape=(out, out), in_specs=[smem] + [hbm...]
    unnamed x6 -> x4, local copies, waits for them, and re-layouts: 12 us -> 12 us
where the time goes in v1:
time: 252 us; the launch traced here: 250 us
  Pallas kernels  237 us (94%)
  local copies, waits for them, and re-layouts  12 us (5%)
    pallas_call x1, Pallas kernels, fused(): pl.pallas_call(fused_kernel, out_shape=(out, out), in_specs=[smem] + [hbm...  237 us
    unnamed x4, local copies, waits for them, and re-layouts  12 us

profile of v1, /device:TPU:0, one launch (start us, length us, event | category | flops | bytes accessed | tf_op | source)
XLA Modules:
  0.0 249.9 jit_solution(6535550037519331687)
XLA Ops:
  0.6 237.2 %shard_map.68 = (f32[2048,1024]{1,0:T(8,128)}, f32[2048,1024]{1,0:T(8,128)}) custom-call(s32[6]{0:T(128)} %starts_ref.1, bf16[512,1024]{1,0:T(8,128)(2,1)} %q_ref.1, bf16[512,1024]{1,0:T(8,128)(2,1)} %k_ref.1, bf16[512,1024]{1,0:T(8,128)(2,1)} %v_ref.1, bf16[512,1024]{1,0:T(8,128)(2,1)} %g_ref.1), custom_call_target="tpu_custom_call" | custom-call | tf_op jit(solution)/shard_map/pallas_call | solution.py:648
  237.9 0.0 copy-start
  237.9 8.6 %copy.9 = f32[2048,1024]{1,0:T(8,128)} copy(f32[2048,1024]{1,0:T(8,128)} %get-tuple-element.4) | data formatting | bytes 16777216
  246.5 0.0 copy-done
  246.5 3.4 %copy.10 = f32[2048,1024]{1,0:T(8,128)} copy(f32[2048,1024]{1,0:T(8,128)S(1)} %copy-done) | data formatting | bytes 16777216
Async XLA Ops:
  237.9 8.6 %copy-start = (f32[2048,1024]{1,0:T(8,128)S(1)}, f32[2048,1024]{1,0:T(8,128)}, u32[]{:S(2)}) copy-start(f32[2048,1024]{1,0:T(8,128)} %get-tuple-element.5) | copy-start | bytes 25165828

commit v2 on v1

--- a/solution.py
+++ b/solution.py
@@ -157,9 +157,9 @@
 
 def fused_kernel(
     starts_ref, q_ref, k_ref, v_ref, g_ref, out_a, out_g,
-    xin, rows, cols, v_t, g_acc, key_doc, query_doc, stage,
+    xin, rows, cols, v_t, g_acc, key_doc, query_doc,
     a2a_send, a2a_recv, row_recv, up_send, down_send, x_send, chunk_send, swap_send,
-    col_recv, pair_send, y_send, relay_send, out_sem,
+    col_recv, pair_send, y_send, relay_send,
 ):
     n = lax.axis_size("tokens")
     tok_dev = q_ref.shape[0]
@@ -407,22 +407,9 @@
         def _():
             cols[j, f, zs] = rows[j, f, x, zs]
 
-    used = [0]
     wide = 2 * HEAD_DIM
-    slots = stage.shape[0]
-
-    def out_copy(f, row, col, slot):
-        return pltpu.make_async_copy(
-            stage.at[slot],
-            (out_a, out_g)[f].at[
-                pl.ds(pl.multiple_of(row * wide, wide), wide),
-                pl.ds(pl.multiple_of(col * wide, wide), wide),
-            ],
-            out_sem.at[slot],
-        )
 
     def products(f, xs, left, right):
-        done = used[0]
         count = len(left) * len(right)
 
         def one(i, carry):
@@ -431,24 +418,16 @@
             pr = sum(((at_left == k) * item[1] for k, item in enumerate(left)), 0)
             jc = sum(((at_right == k) * item[0] for k, item in enumerate(right)), 0)
             pc = sum(((at_right == k) * item[1] for k, item in enumerate(right)), 0)
-            slot = (done + i) % slots
-
-            @pl.when(done + i >= slots)
-            def _():
-                out_copy(f, 0, 0, slot).wait()
-
-            stage[slot] = (
-                lax.dot_general(
-                    rows[jr, f, xs, pl.ds(2 * pr, 2)].reshape(wide, all_tokens),
-                    cols[jc, f, pl.ds(2 * pc, 2)].reshape(wide, all_tokens),
-                    (((1,), (1,)), ((), ())), preferred_element_type=F32,
-                ) * (1.0 / all_tokens)
-            ).astype(stage.dtype)
-            out_copy(f, 4 * xs + 2 * jr + pr, 2 * jc + pc, slot).start()
+            row = pl.multiple_of((4 * xs + 2 * jr + pr) * wide, wide)
+            col = pl.multiple_of((2 * jc + pc) * wide, wide)
+            (out_a, out_g)[f][pl.ds(row, wide), pl.ds(col, wide)] = lax.dot_general(
+                rows[jr, f, xs, pl.ds(2 * pr, 2)].reshape(wide, all_tokens),
+                cols[jc, f, pl.ds(2 * pc, 2)].reshape(wide, all_tokens),
+                (((1,), (1,)), ((), ())), preferred_element_type=F32,
+            ) * (1.0 / all_tokens)
             return carry
 
         lax.fori_loop(0, count, one, 0)
-        used[0] += count
 
     for a in (KEY, VALUE):
         send_inputs(0, (a,), (END, ACROSS))
@@ -586,9 +565,6 @@
     products(1, other_x, (second,), (first, second, last, final))
     other_rows(1, 1, (ACROSS, END))
     products(1, other_x, (final,), (first, second, last, final))
-    for slot in range(slots):
-        out_copy(0, 0, 0, slot).wait()
-
     for j in range(2):
         for a in range(4):
             for source in range(3):
@@ -644,12 +620,12 @@
     dma = pltpu.SemaphoreType.DMA
     hbm = pl.BlockSpec(memory_space=pl.ANY)
     smem = pl.BlockSpec(memory_space=pltpu.SMEM)
-    out = jax.ShapeDtypeStruct((2 * row_width, row_width), F32)
+    out = pltpu.VMEM((2 * row_width, row_width), F32)
     return tuple(pl.pallas_call(
         fused_kernel,
         out_shape=(out, out),
         in_specs=[smem] + [hbm] * 4,
-        out_specs=[hbm] * 2,
+        out_specs=[pl.BlockSpec(memory_space=pltpu.VMEM)] * 2,
         scratch_shapes=[
             pltpu.VMEM((2, 4, all_tokens, HEAD_DIM), BF16),
             pltpu.VMEM((2, 2, 2, n, HEAD_DIM, all_tokens), BF16),
@@ -658,13 +634,12 @@
             pltpu.VMEM((all_tokens, HEAD_DIM), F32),
             pltpu.VMEM((all_tokens, 1), jnp.int32),
             pltpu.VMEM((1, all_tokens), jnp.int32),
-            pltpu.VMEM((8, 2 * HEAD_DIM, 2 * HEAD_DIM), F32),
             dma((2, 4, 3)), dma((2, 4, n)), dma((2, 2, 2, n, 2)),
             dma((2, 2, 2, n)), dma((2, 2, 2, n)), dma((2, 2, 2, n)), dma((n,)), dma((2, 2, 2)),
-            dma((2, 2, n)), dma((2, 2, n)), dma((2, 2, n)), dma((2, 2, n)), dma((8,)),
+            dma((2, 2, n)), dma((2, 2, n)), dma((2, 2, n)), dma((2, 2, n)),
         ],
         compiler_params=pltpu.CompilerParams(
-            collective_id=0, has_side_effects=True, vmem_limit_bytes=60 * 1024 * 1024
+            collective_id=0, has_side_effects=True, vmem_limit_bytes=38 * 1024 * 1024
         ),
     )(doc_starts, query_in, key_in, value_in, out_grads))
 

time: 252 us -> 246 us (0.976)
  local copies, waits for them, and re-layouts: 12 us -> 6.8 us
    unnamed x4 -> x2, local copies, waits for them, and re-layouts: 12 us -> 6.8 us
where the time goes in v2:
time: 246 us; the launch traced here: 244 us
  Pallas kernels  236 us (96%)
  local copies, waits for them, and re-layouts  6.8 us (3%)
    pallas_call x1, Pallas kernels, fused(): pl.pallas_call(fused_kernel, out_shape=(out, out), in_specs=[smem] + [hbm...  236 us
    unnamed x2, local copies, waits for them, and re-layouts  6.8 us

profile of v2, /device:TPU:0, one launch (start us, length us, event | category | flops | bytes accessed | tf_op | source)
XLA Modules:
  0.0 243.9 jit_solution(16797580311679757448)
XLA Ops:
  0.6 236.4 %shard_map.68 = (f32[2048,1024]{1,0:T(8,128)S(1)}, f32[2048,1024]{1,0:T(8,128)S(1)}) custom-call(s32[6]{0:T(128)} %starts_ref.1, bf16[512,1024]{1,0:T(8,128)(2,1)} %q_ref.1, bf16[512,1024]{1,0:T(8,128)(2,1)} %k_ref.1, bf16[512,1024]{1,0:T(8,128)(2,1)} %v_ref.1, bf16[512,1024]{1,0:T(8,128)(2,1)} %g_ref.1), custom_call_target="tpu_custom_call" | custom-call | tf_op jit(solution)/shard_map/pallas_call | solution.py:624
  237.1 3.4 %copy.9 = f32[2048,1024]{1,0:T(8,128)} copy(f32[2048,1024]{1,0:T(8,128)S(1)} %get-tuple-element.2) | data formatting | bytes 16777216
  240.5 3.4 %copy.10 = f32[2048,1024]{1,0:T(8,128)} copy(f32[2048,1024]{1,0:T(8,128)S(1)} %get-tuple-element.3) | data formatting | bytes 16777216

commit v3 on v2

--- a/solution.py
+++ b/solution.py
@@ -207,6 +207,7 @@
         pltpu.make_async_copy(block, block, a2a_recv.at[j, a, position]).wait()
 
     middle = (z > 0) & (z < n - 1)
+    mate = sources[MATE]
 
     def send_inputs(j, kinds, targets):
         for source in targets:
@@ -217,14 +218,21 @@
         for a in kinds:
             own_copy(j, a).start()
 
+    def send_far(j, kinds):
+        @pl.when(middle)
+        def _():
+            send_inputs(j, kinds, (END, ACROSS))
+
+        @pl.when(jnp.logical_not(middle))
+        def _():
+            send_inputs(j, kinds, (ACROSS, END))
+
     def send_next(kinds):
         @pl.when(jnp.logical_not(middle))
         def _():
             send_inputs(1, kinds, (MATE,))
 
-        for a in kinds:
-            for source in (END, ACROSS):
-                a2a_copy(1, a, source).start()
+        send_far(1, kinds)
 
     def chunk_copy(position):
         piece = rows.at[0, 0, x, z, :, token_span(position)]
@@ -243,7 +251,8 @@
         g_acc[...] = jnp.zeros_like(g_acc)
 
         def step(i, carry):
-            position = jnp.where(i == 0, z, jnp.where(i == 1, sources[MATE], jnp.where(i == 2, sources[ACROSS], sources[END])))
+            far_first = (i == 2) == middle
+            position = jnp.where(i == 0, z, jnp.where(i == 1, mate, jnp.where(far_first, sources[END], sources[ACROSS])))
 
             @pl.when(i == 2)
             def _():
@@ -285,7 +294,6 @@
         )
 
     over_x = {"cols": other_x}
-    mate = sources[MATE]
 
     def up_copy(j, f, part, zs):
         return row_copy(j, f, x, zs, part, up_send.at[j, f, part, zs], {"tokens": (z + 1) % n})
@@ -299,19 +307,29 @@
     def swap_copy(j, f, part):
         return row_copy(j, f, other_x, z, part, swap_send.at[j, f, part], {"tokens": mate})
 
-    def own_rows(j, f):
+    def own_rows(j, f, later=False):
         for part in range(2):
-            @pl.when(z < n - 1)
+            @pl.when((z < n - 1) & (z != n // 2 - 1) if later else z < n - 1)
             def _():
                 up_copy(j, f, part, z).start()
 
-            @pl.when(z > 0)
+            @pl.when((z > 0) & (z != n // 2) if later else z > 0)
             def _():
                 down_copy(j, f, part, z).start()
 
             if (j, f) != (0, 0):
                 x_copy(j, f, part, z).start()
         feed_cols(j, f, z)
+
+    def own_inward(j, f):
+        for part in range(2):
+            @pl.when(z == n // 2 - 1)
+            def _():
+                up_copy(j, f, part, z).start()
+
+            @pl.when(z == n // 2)
+            def _():
+                down_copy(j, f, part, z).start()
 
     def rows_in(j, f, source):
         zs = sources[source]
@@ -442,8 +460,7 @@
     for position in (z,) + sources:
         arrived(0, KEY, position)
     send_inputs(0, (QUERY, GRAD), (MATE,))
-    for a in (QUERY, GRAD):
-        send_inputs(0, (a,), (END, ACROSS))
+    send_far(0, (QUERY, GRAD))
 
     @pl.when(middle)
     def _():
@@ -494,7 +511,7 @@
     first, last = (0, near), (0, 1 - near)
     second, final = (1, near), (1, 1 - near)
     own_rows(1, 0)
-    own_rows(1, 1)
+    own_rows(1, 1, later=True)
     in_middle(0, 1)
     at_ends(1, 0)
     end_swap(0, 0)
@@ -502,6 +519,7 @@
     at_ends(1, 1)
     rows_in(0, 0, ACROSS)
     in_middle(1, 0)
+    own_inward(1, 1)
     end_swap(1, 0)
     rows_in(0, 1, ACROSS)
     in_middle(1, 1)
@@ -514,46 +532,46 @@
     cols_pair(0, 0, (None, MATE))
     cols_pair(1, 0, (None, MATE))
     products(0, x, (first, second), (first, second))
-    rows_in(0, 1, END)
+    rows_in(1, 0, ACROSS)
     relay_pair(0, 0, (ACROSS,))
     relay_pair(0, 1, (ACROSS,))
     relay_pair(1, 1, (MATE,))
     cols_pair(0, 1, (None, MATE))
     cols_pair(1, 1, (None, MATE))
     products(1, x, (first, second), (first, second))
-    rows_in(1, 0, ACROSS)
+    rows_in(0, 1, END)
     relay_pair(0, 0, (END,))
     cols_pair(0, 0, (ACROSS, END))
     products(0, x, (last,), (first, second, last))
     products(0, x, (first, second), (last,))
-    rows_in(1, 1, ACROSS)
+    relay_pair(1, 0, (ACROSS,))
+    rows_in(1, 0, END)
     relay_pair(0, 1, (END,))
-    relay_pair(1, 0, (ACROSS,))
+    other_rows(0, 0, (MATE,))
+    other_rows(1, 0, (MATE,))
+    products(0, other_x, (first, second), (first, second, last))
     cols_pair(0, 1, (ACROSS, END))
     products(1, x, (last,), (first, second, last))
     products(1, x, (first, second), (last,))
-    other_rows(0, 0, (MATE,))
-    other_rows(1, 0, (MATE,))
-    products(0, other_x, (first, second), (first, second, last))
-    rows_in(1, 0, END)
-    relay_pair(1, 1, (ACROSS,))
+    rows_in(1, 1, ACROSS)
+    relay_pair(1, 0, (END,))
     other_rows(0, 1, (MATE,))
     products(1, other_x, (first,), (first, second, last))
-    other_rows(0, 0, (ACROSS, END))
-    products(0, other_x, (last,), (first, second, last))
-    relay_pair(1, 0, (END,))
     cols_pair(1, 0, (ACROSS, END))
     products(0, x, (final,), (first, second, last, final))
     products(0, x, (first, second, last), (final,))
+    products(0, other_x, (first, second), (final,))
+    other_rows(0, 0, (ACROSS, END))
+    products(0, other_x, (last,), (first, second, last, final))
+    other_rows(0, 1, (ACROSS, END))
+    products(1, other_x, (last,), (first, second, last))
     rows_in(1, 1, END)
 
     @pl.when(middle)
     def _():
         swap_to_end()
 
-    products(0, other_x, (first, second, last), (final,))
-    other_rows(0, 1, (ACROSS, END))
-    products(1, other_x, (last,), (first, second, last))
+    relay_pair(1, 1, (ACROSS,))
     products(1, x, (final,), (first, second, last))
     relay_pair(1, 1, (END,))
     other_rows(1, 0, (ACROSS, END))

time: 246 us -> 244 us (level)
  no operation moved by 1% of the time
where the time goes in v3:
time: 244 us; the launch traced here: 243 us
  Pallas kernels  236 us (97%)
  local copies, waits for them, and re-layouts  6.8 us (3%)
    pallas_call x1, Pallas kernels, fused(): pl.pallas_call(fused_kernel, out_shape=(out, out), in_specs=[smem] + [hbm...  236 us
    unnamed x2, local copies, waits for them, and re-layouts  6.8 us

profile of v3, /device:TPU:0, one launch (start us, length us, event | category | flops | bytes accessed | tf_op | source)
XLA Modules:
  0.0 243.5 jit_solution(17658923083999176943)
XLA Ops:
  0.6 236.0 %shard_map.68 = (f32[2048,1024]{1,0:T(8,128)S(1)}, f32[2048,1024]{1,0:T(8,128)S(1)}) custom-call(s32[6]{0:T(128)} %starts_ref.1, bf16[512,1024]{1,0:T(8,128)(2,1)} %q_ref.1, bf16[512,1024]{1,0:T(8,128)(2,1)} %k_ref.1, bf16[512,1024]{1,0:T(8,128)(2,1)} %v_ref.1, bf16[512,1024]{1,0:T(8,128)(2,1)} %g_ref.1), custom_call_target="tpu_custom_call" | custom-call | tf_op jit(solution)/shard_map/pallas_call | solution.py:642
  236.7 3.4 %copy.9 = f32[2048,1024]{1,0:T(8,128)} copy(f32[2048,1024]{1,0:T(8,128)S(1)} %get-tuple-element.2) | data formatting | bytes 16777216
  240.1 3.4 %copy.10 = f32[2048,1024]{1,0:T(8,128)} copy(f32[2048,1024]{1,0:T(8,128)S(1)} %get-tuple-element.3) | data formatting | bytes 16777216

commit v4 on v3

--- a/solution.py
+++ b/solution.py
@@ -319,7 +319,7 @@
 
             if (j, f) != (0, 0):
                 x_copy(j, f, part, z).start()
-        feed_cols(j, f, z)
+            feed_cols(j, f, z, part)
 
     def own_inward(j, f):
         for part in range(2):
@@ -350,7 +350,7 @@
                 @pl.when(jnp.logical_not(middle))
                 def _():
                     x_copy(j, f, part, zs).start()
-        feed_cols(j, f, zs)
+            feed_cols(j, f, zs, part)
 
     def other_in(j, f, source, part):
         zs = z if source is None else sources[source]
@@ -385,41 +385,45 @@
     is_source = h == z
     far = y != z // 2
 
-    def col_copy(j, f, zs, source, send, device):
+    def col_copy(j, f, zs, part, source, send, device):
+        span = pl.ds(part * half, half)
         return pltpu.make_async_remote_copy(
-            src_ref=source, dst_ref=cols.at[j, f, zs], send_sem=send.at[j, f, zs],
-            recv_sem=col_recv.at[j, f, zs], device_id={"heads": device},
+            src_ref=source.at[span, :], dst_ref=cols.at[j, f, zs, span, :],
+            send_sem=send.at[j, f, zs, part], recv_sem=col_recv.at[j, f, zs, part],
+            device_id={"heads": device},
         )
 
-    def pair_copy(j, f, zs):
-        return col_copy(j, f, zs, rows.at[j, f, x, zs], pair_send, pair)
-
-    def y_copy(j, f, zs):
-        return col_copy(j, f, zs, rows.at[j, f, x, zs], y_send, (1 - y) * 2 + zs % 2)
-
-    def relay_copy(j, f, zs):
-        return col_copy(j, f, zs, cols.at[j, f, zs], relay_send, pair)
-
-    def feed_cols(j, f, zs):
+    def pair_copy(j, f, zs, part):
+        return col_copy(j, f, zs, part, rows.at[j, f, x, zs], pair_send, pair)
+
+    def y_copy(j, f, zs, part):
+        return col_copy(j, f, zs, part, rows.at[j, f, x, zs], y_send, (1 - y) * 2 + zs % 2)
+
+    def relay_copy(j, f, zs, part):
+        return col_copy(j, f, zs, part, cols.at[j, f, zs], relay_send, pair)
+
+    def feed_cols(j, f, zs, part):
         @pl.when(is_source)
         def _():
-            y_copy(j, f, zs).start()
-            pair_copy(j, f, zs).start()
+            y_copy(j, f, zs, part).start()
+            pair_copy(j, f, zs, part).start()
 
     def relay_cols(j, f, source):
         zs = z if source is None else sources[source]
 
         @pl.when(far & (core == zs % 2))
         def _():
-            relay_copy(j, f, zs).wait_recv()
-            relay_copy(j, f, zs).start()
+            for part in range(2):
+                relay_copy(j, f, zs, part).wait_recv()
+                relay_copy(j, f, zs, part).start()
 
     def cols_in(j, f, source):
         zs = z if source is None else sources[source]
 
         @pl.when(jnp.logical_not(is_source | (far & (core == zs % 2))))
         def _():
-            relay_copy(j, f, zs).wait_recv()
+            for part in range(2):
+                relay_copy(j, f, zs, part).wait_recv()
 
         @pl.when(is_source)
         def _():
@@ -612,14 +616,15 @@
 
                 lax.fori_loop(0, n, sent, 0)
             for zs in range(n):
-                @pl.when(is_source)
-                def _():
-                    pair_copy(j, f, zs).wait_send()
-                    y_copy(j, f, zs).wait_send()
-
-                @pl.when(far & (core == zs % 2))
-                def _():
-                    relay_copy(j, f, zs).wait_send()
+                for part in range(2):
+                    @pl.when(is_source)
+                    def _():
+                        pair_copy(j, f, zs, part).wait_send()
+                        y_copy(j, f, zs, part).wait_send()
+
+                    @pl.when(far & (core == zs % 2))
+                    def _():
+                        relay_copy(j, f, zs, part).wait_send()
     for j in range(2):
         for f in range(2):
             for part in range(2):
@@ -631,6 +636,24 @@
                         swap_copy(j, f, part).wait_send()
 
 
+WRITES = 8
+
+
+def write_kernel(a_ref, g_ref, out_a, out_g, sem):
+    rows = a_ref.shape[0] // WRITES
+    copies = [
+        pltpu.make_async_copy(
+            source.at[pl.ds(k * rows, rows), :], target.at[pl.ds(k * rows, rows), :], sem.at[f, k]
+        )
+        for k in range(WRITES)
+        for f, (source, target) in enumerate(((a_ref, out_a), (g_ref, out_g)))
+    ]
+    for copy in copies:
+        copy.start()
+    for copy in copies:
+        copy.wait()
+
+
 def fused(query_in, key_in, value_in, out_grads, doc_starts):
     n = lax.axis_size("tokens")
     tok_dev, row_width = query_in.shape
@@ -639,7 +662,7 @@
     hbm = pl.BlockSpec(memory_space=pl.ANY)
     smem = pl.BlockSpec(memory_space=pltpu.SMEM)
     out = pltpu.VMEM((2 * row_width, row_width), F32)
-    return tuple(pl.pallas_call(
+    factors = pl.pallas_call(
         fused_kernel,
         out_shape=(out, out),
         in_specs=[smem] + [hbm] * 4,
@@ -654,12 +677,21 @@
             pltpu.VMEM((1, all_tokens), jnp.int32),
             dma((2, 4, 3)), dma((2, 4, n)), dma((2, 2, 2, n, 2)),
             dma((2, 2, 2, n)), dma((2, 2, 2, n)), dma((2, 2, 2, n)), dma((n,)), dma((2, 2, 2)),
-            dma((2, 2, n)), dma((2, 2, n)), dma((2, 2, n)), dma((2, 2, n)),
+            dma((2, 2, n, 2)), dma((2, 2, n, 2)), dma((2, 2, n, 2)), dma((2, 2, n, 2)),
         ],
         compiler_params=pltpu.CompilerParams(
             collective_id=0, has_side_effects=True, vmem_limit_bytes=38 * 1024 * 1024
         ),
-    )(doc_starts, query_in, key_in, value_in, out_grads))
+    )(doc_starts, query_in, key_in, value_in, out_grads)
+    final = jax.ShapeDtypeStruct((2 * row_width, row_width), F32)
+    return tuple(pl.pallas_call(
+        write_kernel,
+        out_shape=(final, final),
+        in_specs=[pl.BlockSpec(memory_space=pltpu.VMEM)] * 2,
+        out_specs=[hbm] * 2,
+        scratch_shapes=[dma((2, WRITES))],
+        compiler_params=pltpu.CompilerParams(vmem_limit_bytes=20 * 1024 * 1024),
+    )(*factors))
 
 
 def per_device(query_in, key_in, value_in, out_grads, doc_starts):

time: 244 us -> 244 us (level)
  Pallas kernels: 236 us -> 243 us
  local copies, waits for them, and re-layouts: 6.8 us -> 0 us
    unnamed x2 -> x0, local copies, waits for them, and re-layouts: 6.8 us -> none
    pallas_call x0 -> x1, Pallas kernels: none -> 5.96 us  [fused(): pl.pallas_call(write_kernel, out_shape=(final, final), in_specs=[pl.Block...]
where the time goes in v4:
time: 244 us; the launch traced here: 243 us
  Pallas kernels  243 us (100%)
    pallas_call x1, Pallas kernels, fused(): pl.pallas_call(fused_kernel, out_shape=(out, out), in_specs=[smem] + [hbm...  237 us
    pallas_call x1, Pallas kernels, fused(): pl.pallas_call(write_kernel, out_shape=(final, final), in_specs=[pl.Block...  5.96 us

profile of v4, /device:TPU:0, one launch (start us, length us, event | category | flops | bytes accessed | tf_op | source)
XLA Modules:
  0.0 243.4 jit_solution(2282724961974918029)
XLA Ops:
  0.6 236.6 %shard_map.68 = (f32[2048,1024]{1,0:T(8,128)S(1)}, f32[2048,1024]{1,0:T(8,128)S(1)}) custom-call(s32[6]{0:T(128)} %starts_ref.1, bf16[512,1024]{1,0:T(8,128)(2,1)} %q_ref.1, bf16[512,1024]{1,0:T(8,128)(2,1)} %k_ref.1, bf16[512,1024]{1,0:T(8,128)(2,1)} %v_ref.1, bf16[512,1024]{1,0:T(8,128)(2,1)} %g_ref.1), custom_call_target="tpu_custom_call" | custom-call | tf_op jit(solution)/shard_map/pallas_call | solution.py:665
  237.3 6.0 %shard_map.69 = (f32[2048,1024]{1,0:T(8,128)}, f32[2048,1024]{1,0:T(8,128)}) custom-call(f32[2048,1024]{1,0:T(8,128)S(1)} %get-tuple-element.4.a_ref, f32[2048,1024]{1,0:T(8,128)S(1)} %get-tuple-element.5.g_ref), custom_call_target="tpu_custom_call" | custom-call | tf_op jit(solution)/shard_map/pallas_call | solution.py:687
